TPU v7x, 32 devices: a whole 2x2x4 slice. The times are simulated.
32 devices in a mesh: tm: 32 (over z, y, x, core).
Axes of the slice: x: 2, y: 2, z: 4, core: 2. Of those that a mesh axis runs over, the one named last changes fastest.
Arguments:
- prior_mean: float32 [128], replicated, may hold values from -6 to 6
- rates: float32 [64], replicated, may hold values from 0.00390625 to 0.3
- observed: float32 [512, 64], P('tm'), may hold values from -6 to 6
- mask: int32 [512, 64], P('tm'), may hold values 0 or 1
- gains: bfloat16 [512, 128, 64], P('tm'), may hold values from -0.3 to 0.3
- smooth_gains: bfloat16 [512, 128, 128], P('tm'), may hold values from -0.1 to 1
- weights: bfloat16 [512, 64, 64], P('tm'), may hold values from -0.1 to 3.5, as said below
Outputs:
- filtered: float32 [512, 128], P('tm')
- smoothed: float32 [512, 128], P('tm')
- fit: float32 [], replicated
Inputs may be any that keep to these rules, and one draw needn't show every extreme that they name: `weights`: symmetric.
All inputs are finite; a program needn't handle non-finite values. No bound on the sum of `mask` on one device may be relied on, other than what follows from the above.
Results may differ from a plain program's by a relative error of at most 0.0003.
Values sent between devices are 32-bit elements; how exact they have to be, the bound alone decides.
A program may use at most 64 MiB of HBM per device.

v0:
```python
import functools
import jax
import jax.numpy as jnp
from jax import lax
from jax.experimental import pallas as pl
from jax.experimental.pallas import tpu as pltpu
from jax.sharding import PartitionSpec as P

F32 = jnp.float32
BF16 = jnp.bfloat16
MESH = pl.DeviceIdType.MESH
PAD = 16


def split(x):
    high = x.astype(BF16)
    return high, (x - high.astype(F32)).astype(BF16)


def dot_nt(a, b):
    return lax.dot_general(a, b, (((1,), (1,)), ((), ())), preferred_element_type=F32)


def dot_nn(a, b):
    return jnp.dot(a, b, preferred_element_type=F32)


def product(a, b):
    a_high, a_low = split(a)
    b_high, b_low = split(b)
    both = jnp.concatenate([a_high, a_low], axis=1)
    twice = jnp.concatenate([b_high, b_high], axis=0)
    return dot_nn(both, twice) + dot_nn(a_high, b_low)


def column(row, state):
    return jnp.transpose(jnp.broadcast_to(row, (state, state)))


def through(col, mat):
    return jnp.sum(col * mat, axis=0, keepdims=True)


def kernel(devices, prior_ref, rates_ref, obs_ref, mask_ref, gain_ref, back_ref, weight_ref,
           filt_ref, smooth_ref, fit_ref,
           coef, obs_s, mask_s, fwd, bwd, cum, fold_f, fold_b, got_f, got_b, vec_out,
           top_out, top_in, msg, got_m, pre, suf, lead,
           fs, fr, bs, br, ms, mr, ts, tr):
    steps, sites, state = gain_ref.shape
    levels = (devices - 1).bit_length()
    me = lax.axis_index("tm")
    bits = [lax.rem(lax.div(me, 1 << k), 2) for k in range(levels)]
    peers = [me + (1 - 2 * bits[k]) * (1 << k) for k in range(levels)]

    barrier = pltpu.get_barrier_semaphore()
    everyone = [sum([(1 - 2 * bits[k]) * (1 << k) for k in range(levels) if j >> k & 1], me) for j in range(devices)]
    for j in range(1, devices):
        pl.semaphore_signal(barrier, inc=1, device_id=(everyone[j],), device_id_type=MESH)

    coef[0:1, 0:sites] = rates_ref[...]
    coef[0:1, sites:state] = rates_ref[...]
    rate = coef[0:1, :]
    lane = lax.broadcasted_iota(jnp.int32, (1, state), 1)
    sign = jnp.where(lane < sites, 1.0, -1.0).astype(F32)
    decay = jnp.exp(-rate)
    same = decay * (1.0 + sign * rate)
    cross = sign * decay * rate

    def predict(x):
        return x * same + pltpu.roll(x, sites, 1) * cross

    obs_s[...] = jnp.zeros_like(obs_s)
    mask_s[...] = jnp.zeros_like(mask_s)
    obs_s[:, 0:sites] = obs_ref[...]
    mask_s[:, 0:sites] = mask_ref[...].astype(F32)

    last = jnp.where(me == devices - 1, 0.0, 1.0).astype(F32)

    def back_twin(t):
        j = back_ref[t]
        if t == steps - 1:
            j = (j.astype(F32) * last).astype(BF16)
        return jnp.concatenate([j, j], axis=1)

    rows = state + PAD
    row = lax.broadcasted_iota(jnp.int32, (rows, state), 0)
    col = lax.broadcasted_iota(jnp.int32, (rows, state), 1)
    is_off = row >= state
    x = jnp.where(row == col, 1.0, 0.0).astype(F32)
    eye = x
    y = x[:state]
    for i in range(steps):
        pred = predict(x)
        seen = mask_s[i:i + 1, :] * (jnp.where(is_off, obs_s[i:i + 1, :], 0.0) - pred)
        high = seen.astype(BF16).astype(F32)
        pair = high + pltpu.roll(seen - high, sites, 1)
        x = pred + dot_nn(pair.astype(BF16), jnp.concatenate([gain_ref[i], gain_ref[i]], axis=0))
        fwd[i] = x
        t = steps - 1 - i
        high, low = split(y)
        y = dot_nt(jnp.concatenate([high, low], axis=1), back_twin(t))
        bwd[t] = y

    def remote(src, dst, send, recv, k):
        return pltpu.make_async_remote_copy(src_ref=src, dst_ref=dst, send_sem=send.at[k], recv_sem=recv.at[k],
                                            device_id=(peers[k],), device_id_type=MESH)

    pl.semaphore_wait(barrier, devices - 1)
    copies = []
    f_copy = remote(fwd.at[steps - 1], got_f.at[0], fs, fr, 0)
    f_copy.start()
    b_copy = remote(bwd.at[0], got_b.at[0], bs, br, 0)
    b_copy.start()
    copies += [f_copy, b_copy]

    u = jnp.zeros((rows, state), F32)
    t_next = steps - 1
    share = -(-steps // (levels - 1))
    f_tot, b_tot = x, y
    for k in range(levels - 1):
        for _ in range(share):
            if t_next >= 0:
                t = t_next
                here = fwd[t]
                high, low = split(u - predict(here))
                u = here + dot_nt(jnp.concatenate([high, low], axis=1), back_twin(t))
                cum[t] = u
                t_next -= 1
        late = bits[k] == 1
        f_copy.wait_recv()
        other = got_f[k]
        first = jnp.where(late, other, f_tot)
        second = jnp.where(late, f_tot, other)
        f_tot = product(first, second[:state]) + jnp.where(is_off, second[state:state + 1], 0.0)
        if k + 1 < levels - 1:
            fold_f[k] = f_tot
            f_copy = remote(fold_f.at[k], got_f.at[k + 1], fs, fr, k + 1)
            f_copy.start()
            copies.append(f_copy)
        else:
            half = through(column(prior_ref[...], state), f_tot[:state]) + f_tot[state:state + 1]
            top_out[...] = jnp.broadcast_to(half, top_out.shape)
            top_copy = pltpu.make_async_remote_copy(
                src_ref=top_out, dst_ref=top_in, send_sem=ts.at[0], recv_sem=tr.at[0],
                device_id=(peers[k + 1],), device_id_type=MESH)
            top_copy.start()
            copies.append(top_copy)
        if k == 0:
            pre[...] = jnp.where(late, other, eye)
        else:
            held = pre[...]
            moved = product(other, held[:state]) + jnp.where(is_off, held[state:state + 1], 0.0)
            pre[...] = jnp.where(late, moved, held)
        b_copy.wait_recv()
        other_b = got_b[k]
        if k + 1 < levels - 1:
            b_tot = product(jnp.where(late, b_tot, other_b), jnp.where(late, other_b, b_tot))
            fold_b[k] = b_tot
            b_copy = remote(fold_b.at[k], got_b.at[k + 1], bs, br, k + 1)
            b_copy.start()
            copies.append(b_copy)
        if k == 0:
            suf[1] = jnp.where(late, eye[:state], other_b)
            lead[1] = jnp.where(late, other_b, eye[:state])
        else:
            joined = product(jnp.where(late, lead[k], other_b), jnp.where(late, other_b, suf[k]))
            suf[k + 1] = jnp.where(late, suf[k], joined)
            lead[k + 1] = jnp.where(late, joined, lead[k])

    top_copy.wait_recv()
    m = jnp.where(bits[levels - 1] == 1, top_in[0:1, :], prior_ref[...])
    m = through(column(m, state), pre[0:state, :]) + pre[state:state + 1, :]

    m_col = column(m, state)
    g = through(m_col, cum[0, 0:state, :]) + cum[0, state:state + 1, :]

    vec_out[0:1, :] = m
    for t in range(steps):
        now = through(m_col, fwd[t, 0:state, :]) + fwd[t, state:state + 1, :]
        filt_ref[t:t + 1, :] = now
        vec_out[t + 1:t + 2, :] = now

    v = mask_s[...] * (obs_s[...] - predict(vec_out[0:steps, :]))
    v_rows = lax.broadcasted_iota(jnp.int32, v.shape, 0)
    acc = jnp.zeros((2 * steps, sites), F32)
    for t in range(steps):
        high, low = split(jnp.where(v_rows == t, v, 0.0))
        acc += dot_nn(jnp.concatenate([high, low], axis=0)[:, 0:sites], weight_ref[t])
    quad = jnp.sum(v[:, 0:sites] * (acc[0:steps] + acc[steps:]), axis=0, keepdims=True)
    q_tot = jnp.sum(quad, axis=1, keepdims=True)
    c_tot = jnp.sum(jnp.sum(mask_s[...], axis=0, keepdims=True), axis=1, keepdims=True)
    g_col = column(g, state)
    for k in range(levels):
        msg[k, 0:1, :] = g if k == 0 else through(g_col, lead[k])
        msg[k, 1:2, :] = jnp.broadcast_to(q_tot, (1, state))
        msg[k, 2:3, :] = jnp.broadcast_to(c_tot, (1, state))
        msg[k, 3:8, :] = jnp.zeros((5, state), F32)
    arrivals = []
    for j in reversed(range(1, devices)):
        copy = pltpu.make_async_remote_copy(
            src_ref=msg.at[j.bit_length() - 1], dst_ref=got_m.at[j], send_sem=ms.at[j], recv_sem=mr.at[j],
            device_id=(everyone[j],), device_id_type=MESH)
        copy.start()
        arrivals.append((j, copy))
        copies.append(copy)
    for t in range(steps):
        smooth_ref[t:t + 1, :] = through(m_col, cum[t, 0:state, :]) + cum[t, state:state + 1, :]
    sums = [jnp.zeros((8, state), F32) for _ in range(levels)]
    for j, copy in reversed(arrivals):
        copy.wait_recv()
        sums[j.bit_length() - 1] += got_m[j]
    h = jnp.where(bits[0] == 1, 0.0, sums[0][0:1])
    for k in range(1, levels):
        h += through(column(jnp.where(bits[k] == 1, 0.0, sums[k][0:1]), state), suf[k])
    s_col = column(h, state)
    for t in range(steps):
        smooth_ref[t:t + 1, :] = smooth_ref[t:t + 1, :] + through(s_col, bwd[t])
    whole = functools.reduce(jnp.add, sums)
    q_tot = q_tot + whole[1:2, 0:1]
    c_tot = c_tot + whole[2:3, 0:1]
    fit_ref[...] = -0.5 * q_tot / jnp.maximum(c_tot, 1.0)
    for c in copies:
        c.wait_send()


def body(devices, prior_mean, rates, observed, mask, gains, smooth_gains, weights):
    steps, state, sites = gains.shape
    levels = (devices - 1).bit_length()
    rows = state + PAD
    vmem = pl.BlockSpec(memory_space=pltpu.VMEM)
    dma = pltpu.SemaphoreType.DMA
    filtered, smoothed, fit = pl.pallas_call(
        functools.partial(kernel, devices),
        out_shape=(jax.ShapeDtypeStruct((steps, state), F32), jax.ShapeDtypeStruct((steps, state), F32),
                   jax.ShapeDtypeStruct((1, 1), F32)),
        in_specs=[vmem] * 7,
        out_specs=(vmem, vmem, vmem),
        scratch_shapes=[
            pltpu.VMEM((8, state), F32),
            pltpu.VMEM((steps, state), F32),
            pltpu.VMEM((steps, state), F32),
            pltpu.VMEM((steps, rows, state), F32),
            pltpu.VMEM((steps, state, state), F32),
            pltpu.VMEM((steps, rows, state), F32),
            pltpu.VMEM((levels, rows, state), F32),
            pltpu.VMEM((levels, state, state), F32),
            pltpu.VMEM((levels, rows, state), F32),
            pltpu.VMEM((levels, state, state), F32),
            pltpu.VMEM((steps + 8, state), F32),
            pltpu.VMEM((8, state), F32),
            pltpu.VMEM((8, state), F32),
            pltpu.VMEM((levels, 8, state), F32),
            pltpu.VMEM((devices, 8, state), F32),
            pltpu.VMEM((rows, state), F32),
            pltpu.VMEM((levels, state, state), F32),
            pltpu.VMEM((levels, state, state), F32),
            dma((levels,)), dma((levels,)), dma((levels,)), dma((levels,)),
            dma((devices,)), dma((devices,)), dma((1,)), dma((1,)),
        ],
        compiler_params=pltpu.CompilerParams(collective_id=0, has_side_effects=True),
        name="smoother",
    )(prior_mean.reshape(1, state), rates.reshape(1, sites), observed, mask, jnp.swapaxes(gains, 1, 2), smooth_gains, weights)
    return filtered, smoothed, fit.reshape(())


def solution(mesh):
    placed = (P(), P(), P("tm", None), P("tm", None), P("tm", None, None), P("tm", None, None), P("tm", None, None))
    return jax.shard_map(
        functools.partial(body, mesh.shape["tm"]),
        mesh=mesh,
        in_specs=placed,
        out_specs=(P("tm", None), P("tm", None), P()),
        check_vma=False,
    )
```

profile of v0, /device:TPU:0, one launch (start us, length us, event | category | flops | bytes accessed | tf_op | source)
XLA Modules:
  0.0 35.9 jit_solution(16557001186165519399)
XLA Ops:
  0.6 31.6 %smoother.1 = (f32[16,128]{1,0:T(8,128)}, f32[16,128]{1,0:T(8,128)}, f32[1,1]{1,0:T(1,128)}) custom-call(f32[1,128]{1,0:T(1,128)} %bitcast.5, f32[1,64]{1,0:T(1,128)} %bitcast.6, f32[16,64]{1,0:T(8,128)} %obs_ref.1, s32[16,64]{1,0:T(8,128)} %mask_ref.1, bf16[16,64,128]{2,1,0:T(8,128)(2,1)} %bitcast.4, bf16[16,128,128]{2,1,0:T(8,128)(2,1)} %back_ref.1, ...), custom_call_target="tpu_custom_call" | custom-call | tf_op jit(solution)/shard_map/smoother/pallas_call | solution.py:232
  32.3 0.0 copy-start
  32.3 1.3 %copy.13 = f32[16,128]{1,0:T(8,128)} copy(f32[16,128]{1,0:T(8,128)} %get-tuple-element.12) | data formatting | bytes 16384
  33.6 0.0 copy-done
  33.6 0.6 %copy.14 = f32[16,128]{1,0:T(8,128)} copy(f32[16,128]{1,0:T(8,128)S(1)} %copy-done) | data formatting | bytes 16384
Async XLA Ops:
  32.3 1.3 %copy-start = (f32[16,128]{1,0:T(8,128)S(1)}, f32[16,128]{1,0:T(8,128)}, u32[]{:S(2)}) copy-start(f32[16,128]{1,0:T(8,128)} %get-tuple-element.13) | copy-start | bytes 24580
where the time goes:
time: 36.2 us; the launch traced here: 35.9 us
  Pallas kernels  31.6 us (87%)
  between operations  2.39 us (7%)
  local copies, waits for them, and re-layouts  1.9 us (5%)
    pallas_call x1, Pallas kernels, body(): pl.pallas_call(functools.partial(kernel, devices), out_shape=(jax.ShapeDt...  31.6 us
    unnamed x4, local copies, waits for them, and re-layouts  1.9 us

commit v1 on v0

--- a/solution.py
+++ b/solution.py
@@ -218,9 +218,15 @@
     whole = functools.reduce(jnp.add, sums)
     q_tot = q_tot + whole[1:2, 0:1]
     c_tot = c_tot + whole[2:3, 0:1]
-    fit_ref[...] = -0.5 * q_tot / jnp.maximum(c_tot, 1.0)
+    fit_ref[...] = jnp.broadcast_to(-0.5 * q_tot / jnp.maximum(c_tot, 1.0), fit_ref.shape)
     for c in copies:
         c.wait_send()
+
+
+def finish(a_ref, b_ref, c_ref, x_ref, y_ref, z_ref):
+    x_ref[...] = a_ref[...]
+    y_ref[...] = b_ref[...]
+    z_ref[...] = c_ref[0:1, 0:1]
 
 
 def body(devices, prior_mean, rates, observed, mask, gains, smooth_gains, weights):
@@ -231,8 +237,8 @@
     dma = pltpu.SemaphoreType.DMA
     filtered, smoothed, fit = pl.pallas_call(
         functools.partial(kernel, devices),
-        out_shape=(jax.ShapeDtypeStruct((steps, state), F32), jax.ShapeDtypeStruct((steps, state), F32),
-                   jax.ShapeDtypeStruct((1, 1), F32)),
+        out_shape=(pltpu.VMEM((steps, state), F32), pltpu.VMEM((steps, state), F32),
+                   pltpu.VMEM((8, state), F32)),
         in_specs=[vmem] * 7,
         out_specs=(vmem, vmem, vmem),
         scratch_shapes=[
@@ -260,6 +266,14 @@
         compiler_params=pltpu.CompilerParams(collective_id=0, has_side_effects=True),
         name="smoother",
     )(prior_mean.reshape(1, state), rates.reshape(1, sites), observed, mask, jnp.swapaxes(gains, 1, 2), smooth_gains, weights)
+    filtered, smoothed, fit = pl.pallas_call(
+        finish,
+        out_shape=(jax.ShapeDtypeStruct((steps, state), F32), jax.ShapeDtypeStruct((steps, state), F32),
+                   jax.ShapeDtypeStruct((1, 1), F32)),
+        in_specs=[vmem] * 3,
+        out_specs=(vmem, vmem, vmem),
+        name="finish",
+    )(*[pltpu.with_memory_space_constraint(a, pltpu.VMEM) for a in (filtered, smoothed, fit)])
     return filtered, smoothed, fit.reshape(())
 
 

time: 36.2 us -> 32.4 us (0.90)
  local copies, waits for them, and re-layouts: 1.9 us -> 0 us
  between operations: 2.39 us -> 0.64 us
    unnamed x4 -> x0, local copies, waits for them, and re-layouts: 1.9 us -> none
    pallas_call x1 -> x2, Pallas kernels: 31.6 us -> 31.6 us  [the longest x1 31 us: body(): pl.pallas_call(functools.partial(kernel, devices), out_shape=(pltpu.VMEM(...]
where the time goes in v1:
time: 32.4 us; the launch traced here: 32.3 us
  Pallas kernels  31.6 us (98%)
  between operations  0.64 us (2%)
    pallas_call x1, Pallas kernels, body(): pl.pallas_call(functools.partial(kernel, devices), out_shape=(pltpu.VMEM(...  31 us

profile of v1, /device:TPU:0, one launch (start us, length us, event | category | flops | bytes accessed | tf_op | source)
XLA Modules:
  0.0 32.3 jit_solution(11338157928911646699)
XLA Ops:
  0.6 31.0 %smoother.1 = (f32[16,128]{1,0:T(8,128)S(1)}, f32[16,128]{1,0:T(8,128)S(1)}, f32[8,128]{1,0:T(8,128)S(1)}) custom-call(f32[1,128]{1,0:T(1,128)} %bitcast.5, f32[1,64]{1,0:T(1,128)} %bitcast.6, f32[16,64]{1,0:T(8,128)} %obs_ref.1, s32[16,64]{1,0:T(8,128)} %mask_ref.1, bf16[16,64,128]{2,1,0:T(8,128)(2,1)} %bitcast.4, bf16[16,128,128]{2,1,0:T(8,128)(2,1)} %back_ref.1, ...), custom_call_target="tpu_custom_call" | custom-call | tf_op jit(solution)/shard_map/smoother/pallas_call | solution.py:238
  31.7 0.6 %finish.1 = (f32[16,128]{1,0:T(8,128)}, f32[16,128]{1,0:T(8,128)}, f32[1,1]{1,0:T(1,128)}) custom-call(f32[16,128]{1,0:T(8,128)S(1)} %get-tuple-element.9.a_ref, f32[16,128]{1,0:T(8,128)S(1)} %get-tuple-element.10.b_ref, f32[8,128]{1,0:T(8,128)S(1)} %get-tuple-element.11.c_ref), custom_call_target="tpu_custom_call" | custom-call | tf_op jit(solution)/shard_map/finish/pallas_call | solution.py:269
